TPU v7x, 32 devices: a whole 2x2x4 slice. The times are simulated.
32 devices in a mesh: tm: 8 (over z, x), chan: 4 (over y, core).
Axes of the slice: x: 2, y: 2, z: 4, core: 2. Of those that a mesh axis runs over, the one named last changes fastest.
Arguments:
- surveillance: bfloat16 [128, 1024, 256], P(('chan', 'tm')), parts along dimension 0, may hold values from -6 to 6
- ref_samples: bfloat16 [32, 1040, 256], P('tm'), may hold values from -6 to 6
- block_ids: int32 [32], P('tm'), may hold values from 0 to 31, each once
- walk: int32 [32], P('tm'), may hold values from 0 to 63
- cfar_guard: int32 [2048], P('tm'), may hold values from 1 to 8
- cfar_window: int32 [2048], P('tm'), may hold values from 1 to 16
Outputs:
- detection: float32 [8192, 512], P(('chan', 'tm')), parts along dimension 0
There are 4 independent parts, one for each index of `chan`. A program takes and returns all parts, laid end to end along the dimension named above; an argument that names none is the same for every part. Nothing has to cross between parts.
Inputs may be any that keep to these rules, and one draw needn't show every extreme that they name: block_ids names each of 0 to 31 exactly once.
All inputs are finite; a program needn't handle non-finite values.
Results may differ from a plain program's by a relative error of at most 0.0003.
Values sent between devices are 32-bit elements; how exact they have to be, the bound alone decides.
No kernel may reach another device: no remote copies, remote signals or barrier semaphores. Data moves between devices by JAX's collectives and lax.ppermute only.
A program may use at most 64 MiB of HBM per device.

v0:
```python
import math
import jax
import jax.numpy as jnp
from jax import lax
from jax.sharding import PartitionSpec as P

D = 2048
DOP = 512
SEGS = 64
GUARD_MAX = 8
WIN_MAX = 16
HIGH = lax.Precision.HIGHEST


def with_halo(x, sides, width):
    for axis, dim in sides:
        count, length = (lax.axis_size(axis), x.shape[dim])
        up = [(i, (i + 1) % count) for i in range(count - 1)]
        down = [(j, i) for i, j in up]
        last = lax.slice_in_dim(x, length - width, length, axis=dim)
        initial = lax.slice_in_dim(x, 0, width, axis=dim)
        before = lax.ppermute(last, axis, up)
        after = lax.ppermute(initial, axis, down)
        x = jnp.concatenate([before, x, after], axis=dim)
    return x


def phase(product, total):
    return 2.0 * math.pi / total * (product % total).astype(jnp.float32)


def square_tables(width):
    place = jnp.arange(width, dtype=jnp.int32)
    theta = phase(place[:, None] * place[None, :], width)
    return (jnp.cos(theta), jnp.sin(theta))


def make_tables():
    length = 2 * D
    rows = length // 128
    small_cos, small_sin = square_tables(rows)
    wide_cos, wide_sin = square_tables(128)
    mixer = jnp.concatenate(
        [jnp.concatenate([wide_cos, -wide_sin], 1), jnp.concatenate([wide_sin, wide_cos], 1)], 0
    )
    first_idx = jnp.arange(rows, dtype=jnp.int32)[:, None]
    second_idx = jnp.arange(128, dtype=jnp.int32)[None, :]
    twist = phase(first_idx * second_idx, length)
    spread = first_idx + rows * second_idx
    return (small_cos, small_sin, jnp.cos(twist), jnp.sin(twist), mixer, spread)


def forward(signal, tables):
    small_cos, small_sin, twist_cos, twist_sin, mixer, spread = tables
    first = jnp.einsum("kn,snc->skc", small_cos, signal, precision=HIGH)
    second = jnp.einsum("kn,snc->skc", small_sin, signal, precision=HIGH)
    real_part = first[..., :128] + second[..., 128:]
    imag_part = first[..., 128:] - second[..., :128]
    turned = jnp.concatenate(
        [
            real_part * twist_cos + imag_part * twist_sin,
            imag_part * twist_cos - real_part * twist_sin,
        ],
        axis=-1,
    )
    return jnp.einsum("skc,cd->skd", turned, mixer, precision=HIGH)


def inverse(spectrum, tables):
    small_cos, small_sin, twist_cos, twist_sin, mixer, spread = tables
    mixed = jnp.dot(spectrum, mixer.T, precision=HIGH)
    real_part = mixed[:, :128]
    imag_part = mixed[:, 128:]
    turned = jnp.concatenate(
        [
            real_part * twist_cos - imag_part * twist_sin,
            imag_part * twist_cos + real_part * twist_sin,
        ],
        axis=-1,
    )
    with_cos = jnp.dot(small_cos, turned, precision=HIGH)
    with_sin = jnp.dot(small_sin, turned, precision=HIGH)
    result = jnp.concatenate(
        [with_cos[:, :128] - with_sin[:, 128:], with_cos[:, 128:] + with_sin[:, :128]], axis=-1
    )
    return result / (2.0 * D)


def correlate(surv_rows, ref_rows, shift, tables):
    seg_rows = D // 128
    rows_all = surv_rows.shape[0]
    segs = rows_all // seg_rows
    echo = surv_rows.astype(jnp.float32).reshape(segs, seg_rows, 256)
    echo = jnp.concatenate([echo, jnp.zeros_like(echo)], axis=1)
    direct = ref_rows.astype(jnp.float32)
    direct = jnp.concatenate(
        [
            direct[:rows_all].reshape(segs, seg_rows, 256),
            direct[seg_rows:].reshape(segs, seg_rows, 256),
        ],
        axis=1,
    )
    echo_hat = forward(echo, tables)
    direct_hat = forward(direct, tables)
    echo_re = echo_hat[..., :128]
    echo_im = echo_hat[..., 128:]
    direct_re = direct_hat[..., :128]
    direct_im = direct_hat[..., 128:]
    spec_re = jnp.sum(echo_re * direct_re + echo_im * direct_im, axis=0)
    spec_im = jnp.sum(echo_im * direct_re - echo_re * direct_im, axis=0)
    ramp = phase(tables[5] * shift, 2 * D)
    ramp_cos = jnp.cos(ramp)
    ramp_sin = jnp.sin(ramp)
    turned = jnp.concatenate(
        [spec_re * ramp_cos + spec_im * ramp_sin, spec_im * ramp_cos - spec_re * ramp_sin], axis=-1
    )
    lagged = inverse(turned, tables)
    picked = lagged[seg_rows:]
    delay_idx = (
        128 * jnp.arange(seg_rows, dtype=jnp.int32)[:, None]
        + (jnp.arange(256, dtype=jnp.int32) % 128)[None, :]
    )
    return jnp.where(delay_idx >= shift, picked, 0.0)


def doppler_mixer(ids, norm):
    freq = jnp.arange(DOP, dtype=jnp.int32)
    theta = phase(ids[:, None] * freq[None, :], DOP)
    cos_table = jnp.cos(theta) * norm
    sin_table = jnp.sin(theta) * norm
    return jnp.concatenate(
        [jnp.concatenate([cos_table, -sin_table], 1), jnp.concatenate([sin_table, cos_table], 1)], 0
    )


def body(surveillance, ref_samples, block_ids, walk, cfar_guard, cfar_window):
    blocks = surveillance.shape[0]
    devices = lax.axis_size("tm")
    total_blocks = blocks * devices
    span = D // devices
    reach = GUARD_MAX + WIN_MAX
    base = lax.axis_index("tm") * span
    tables = make_tables()
    corr = lax.map(
        lambda item: correlate(item[0], item[1], item[2], tables), (surveillance, ref_samples, walk)
    )
    real_c = corr[:, :, :128].reshape(blocks, D)
    imag_c = corr[:, :, 128:].reshape(blocks, D)
    norm = 1.0 / math.sqrt(total_blocks * SEGS * D)
    moved = lax.all_to_all(
        jnp.stack([real_c, imag_c], axis=1), "tm", split_axis=2, concat_axis=0, tiled=True
    )
    ids = lax.all_gather(block_ids, "tm", axis=0, tiled=True)
    stacked = jnp.concatenate([moved[:, 0], moved[:, 1]], 0)
    mixer = doppler_mixer(ids, norm)
    amp = lax.dot_general(stacked, mixer, (((0,), (0,)), ((), ())), precision=HIGH)
    floor = jnp.sum(moved * moved, axis=(0, 1))
    floor = floor / (total_blocks * SEGS * D)
    power = amp[:, :DOP] * amp[:, :DOP] + amp[:, DOP:] * amp[:, DOP:]
    padded = with_halo(power, (("tm", 0),), reach)
    guard = cfar_guard[:, None]
    width = cfar_window[:, None]

    def inside(dist):
        return ((dist > guard) & (dist <= guard + width)).astype(jnp.float32)

    row_idx = jnp.arange(span, dtype=jnp.int32)[:, None]
    col_idx = jnp.arange(span + 2 * reach, dtype=jnp.int32)[None, :]
    band = inside(jnp.abs(col_idx - reach - row_idx))
    spot = base + jnp.arange(span + 2 * reach, dtype=jnp.int32) - reach
    valid = ((spot >= 0) & (spot < D)).astype(jnp.float32)
    delay_sum = jnp.dot(band, padded, precision=HIGH)
    count = jnp.dot(band, valid, precision=HIGH)
    doppler_sum = jnp.zeros_like(power)
    for step in range(1, reach + 1):
        active = inside(jnp.full((1, 1), step, jnp.int32))
        doppler_sum = doppler_sum + active * (
            jnp.roll(power, -step, axis=1) + jnp.roll(power, step, axis=1)
        )
    noise = (delay_sum + doppler_sum) / (count[:, None] + 2.0 * width.astype(jnp.float32))
    return (power - floor[:, None]) / (0.25 + noise)


def solution(mesh):
    in_specs = (
        P(("chan", "tm"), None, None),
        P("tm", None, None),
        P("tm"),
        P("tm"),
        P("tm"),
        P("tm"),
    )
    out_specs = P(("chan", "tm"), None)
    return jax.shard_map(body, mesh=mesh, in_specs=in_specs, out_specs=out_specs, check_vma=False)
```

profile of v0, /device:TPU:0, one launch (start us, length us, event | category | flops | bytes accessed | tf_op | source)
XLA Modules:
  0.0 126.7 jit_solution(17962002947929078072)
XLA Ops:
  0.6 69.0 %while.15 = (s32[]{:T(128)}, f32[4,16,256]{2,1,0:T(8,128)S(1)}, s32[4]{0:T(128)}, bf16[4,1024,256]{2,1,0:T(8,128)(2,1)}, f32[256,256]{1,0:T(8,128)S(1)}, /*index...) while((s32[]{:T(128)}, f32[4,16,256]{2,1,0:T(8,128)S(1)}, s32[4]{0:T(128)}, ...), condition=%wide.region_3.4_spmd.clone.clone, body=%wide.region_0.3_spmd.clone.clone.sunk | while | flops 4067001856 | bytes 47000764 | solution.py:144
  0.6 1.3 %dynamic_slice.37 = s32[1]{0:T(128)} dynamic-slice(s32[4]{0:T(128)} %get-tuple-element.542, s32[]{:T(128)S(6)} %copy.37), dynamic_slice_sizes={1} | dynamic-slice | bytes 12 | tf_op jit(solution)/shard_map/while/body/jit(dynamic_index_in_dim)/dynamic_slice | solution.py:144
  2.0 1.1 constant_dynamic-slice_fusion.2
  3.1 1.1 dynamic-slice_convert_fusion.2
  4.4 2.0 %fusion.285 = f32[64,32,256]{2,1,0:T(8,128)S(1)} fusion(f32[64,16,256]{2,1,0:T(8,128)S(1)} %bitcast.89, f32[64,16,256]{2,1,0:T(8,128)S(1)} %bitcast.87), kind=kOutput, calls=%fused_computation.16.clone.1 | convolution fusion | flops 201865216 | bytes 4194304 | tf_op jit(solution)/shard_map/while/body/eval_jaxpr/kn,snc->skc/dot_general | solution.py:55
  6.4 2.0 %fusion.284 = f32[64,32,256]{2,1,0:T(8,128)S(1)} fusion(f32[64,16,256]{2,1,0:T(8,128)S(1)} %bitcast.90, f32[64,16,256]{2,1,0:T(8,128)S(1)} %bitcast.88), kind=kOutput, calls=%fused_computation.17.clone.1 | convolution fusion | flops 201865216 | bytes 4194304 | tf_op jit(solution)/shard_map/while/body/eval_jaxpr/kn,snc->skc/dot_general | solution.py:56
  8.4 1.0 convolution_bitcast_fusion.9
  9.5 1.0 convolution_bitcast_fusion.8
  11.3 1.9 %fusion.286 = f32[64,32,256]{2,1,0:T(8,128)S(1)} fusion(f32[64,32,128]{2,1,0:T(8,128)S(1)} %get-tuple-element.512, f32[64,32,128]{2,1,0:T(8,128)S(1)} %get-tuple-element.513, f32[256,256]{1,0:T(8,128)S(1)} %get-tuple-element.544), kind=kOutput, calls=%fused_computation.10.clone.1 | convolution fusion | flops 1611137024 | bytes 4456448 | tf_op jit(solution)/shard_map/while/body/eval_jaxpr/skc,cd->skd/dot_general | solution.py:66
  13.2 1.9 %fusion.287 = f32[64,32,256]{2,1,0:T(8,128)S(1)} fusion(f32[64,32,128]{2,1,0:T(8,128)S(1)} %get-tuple-element.514, f32[64,32,128]{2,1,0:T(8,128)S(1)} %get-tuple-element.515, f32[256,256]{1,0:T(8,128)S(1)} %get-tuple-element.544), kind=kOutput, calls=%fused_computation.5.clone.1 | convolution fusion | flops 1611137024 | bytes 4456448 | tf_op jit(solution)/shard_map/while/body/eval_jaxpr/skc,cd->skd/dot_general | solution.py:66
  17.8 1.3 %dynamic_slice.37 = s32[1]{0:T(128)} dynamic-slice(s32[4]{0:T(128)} %get-tuple-element.542, s32[]{:T(128)S(6)} %copy.37), dynamic_slice_sizes={1} | dynamic-slice | bytes 12 | tf_op jit(solution)/shard_map/while/body/jit(dynamic_index_in_dim)/dynamic_slice | solution.py:144
  19.2 1.1 constant_dynamic-slice_fusion.2
  20.3 1.1 dynamic-slice_convert_fusion.2
  21.6 2.0 %fusion.285 = f32[64,32,256]{2,1,0:T(8,128)S(1)} fusion(f32[64,16,256]{2,1,0:T(8,128)S(1)} %bitcast.89, f32[64,16,256]{2,1,0:T(8,128)S(1)} %bitcast.87), kind=kOutput, calls=%fused_computation.16.clone.1 | convolution fusion | flops 201865216 | bytes 4194304 | tf_op jit(solution)/shard_map/while/body/eval_jaxpr/kn,snc->skc/dot_general | solution.py:55
  23.6 2.0 %fusion.284 = f32[64,32,256]{2,1,0:T(8,128)S(1)} fusion(f32[64,16,256]{2,1,0:T(8,128)S(1)} %bitcast.90, f32[64,16,256]{2,1,0:T(8,128)S(1)} %bitcast.88), kind=kOutput, calls=%fused_computation.17.clone.1 | convolution fusion | flops 201865216 | bytes 4194304 | tf_op jit(solution)/shard_map/while/body/eval_jaxpr/kn,snc->skc/dot_general | solution.py:56
  25.7 1.0 convolution_bitcast_fusion.9
  26.7 1.0 convolution_bitcast_fusion.8
  28.5 1.9 %fusion.286 = f32[64,32,256]{2,1,0:T(8,128)S(1)} fusion(f32[64,32,128]{2,1,0:T(8,128)S(1)} %get-tuple-element.512, f32[64,32,128]{2,1,0:T(8,128)S(1)} %get-tuple-element.513, f32[256,256]{1,0:T(8,128)S(1)} %get-tuple-element.544), kind=kOutput, calls=%fused_computation.10.clone.1 | convolution fusion | flops 1611137024 | bytes 4456448 | tf_op jit(solution)/shard_map/while/body/eval_jaxpr/skc,cd->skd/dot_general | solution.py:66
  30.4 1.9 %fusion.287 = f32[64,32,256]{2,1,0:T(8,128)S(1)} fusion(f32[64,32,128]{2,1,0:T(8,128)S(1)} %get-tuple-element.514, f32[64,32,128]{2,1,0:T(8,128)S(1)} %get-tuple-element.515, f32[256,256]{1,0:T(8,128)S(1)} %get-tuple-element.544), kind=kOutput, calls=%fused_computation.5.clone.1 | convolution fusion | flops 1611137024 | bytes 4456448 | tf_op jit(solution)/shard_map/while/body/eval_jaxpr/skc,cd->skd/dot_general | solution.py:66
  35.1 1.3 %dynamic_slice.37 = s32[1]{0:T(128)} dynamic-slice(s32[4]{0:T(128)} %get-tuple-element.542, s32[]{:T(128)S(6)} %copy.37), dynamic_slice_sizes={1} | dynamic-slice | bytes 12 | tf_op jit(solution)/shard_map/while/body/jit(dynamic_index_in_dim)/dynamic_slice | solution.py:144
  36.5 1.1 constant_dynamic-slice_fusion.2
  37.6 1.1 dynamic-slice_convert_fusion.2
  38.9 2.0 %fusion.285 = f32[64,32,256]{2,1,0:T(8,128)S(1)} fusion(f32[64,16,256]{2,1,0:T(8,128)S(1)} %bitcast.89, f32[64,16,256]{2,1,0:T(8,128)S(1)} %bitcast.87), kind=kOutput, calls=%fused_computation.16.clone.1 | convolution fusion | flops 201865216 | bytes 4194304 | tf_op jit(solution)/shard_map/while/body/eval_jaxpr/kn,snc->skc/dot_general | solution.py:55
  40.9 2.0 %fusion.284 = f32[64,32,256]{2,1,0:T(8,128)S(1)} fusion(f32[64,16,256]{2,1,0:T(8,128)S(1)} %bitcast.90, f32[64,16,256]{2,1,0:T(8,128)S(1)} %bitcast.88), kind=kOutput, calls=%fused_computation.17.clone.1 | convolution fusion | flops 201865216 | bytes 4194304 | tf_op jit(solution)/shard_map/while/body/eval_jaxpr/kn,snc->skc/dot_general | solution.py:56
  42.9 1.0 convolution_bitcast_fusion.9
  43.9 1.0 convolution_bitcast_fusion.8
  45.8 1.9 %fusion.286 = f32[64,32,256]{2,1,0:T(8,128)S(1)} fusion(f32[64,32,128]{2,1,0:T(8,128)S(1)} %get-tuple-element.512, f32[64,32,128]{2,1,0:T(8,128)S(1)} %get-tuple-element.513, f32[256,256]{1,0:T(8,128)S(1)} %get-tuple-element.544), kind=kOutput, calls=%fused_computation.10.clone.1 | convolution fusion | flops 1611137024 | bytes 4456448 | tf_op jit(solution)/shard_map/while/body/eval_jaxpr/skc,cd->skd/dot_general | solution.py:66
  47.7 1.9 %fusion.287 = f32[64,32,256]{2,1,0:T(8,128)S(1)} fusion(f32[64,32,128]{2,1,0:T(8,128)S(1)} %get-tuple-element.514, f32[64,32,128]{2,1,0:T(8,128)S(1)} %get-tuple-element.515, f32[256,256]{1,0:T(8,128)S(1)} %get-tuple-element.544), kind=kOutput, calls=%fused_computation.5.clone.1 | convolution fusion | flops 1611137024 | bytes 4456448 | tf_op jit(solution)/shard_map/while/body/eval_jaxpr/skc,cd->skd/dot_general | solution.py:66
  52.3 1.3 %dynamic_slice.37 = s32[1]{0:T(128)} dynamic-slice(s32[4]{0:T(128)} %get-tuple-element.542, s32[]{:T(128)S(6)} %copy.37), dynamic_slice_sizes={1} | dynamic-slice | bytes 12 | tf_op jit(solution)/shard_map/while/body/jit(dynamic_index_in_dim)/dynamic_slice | solution.py:144
  53.7 1.1 constant_dynamic-slice_fusion.2
  54.8 1.1 dynamic-slice_convert_fusion.2
  56.1 2.0 %fusion.285 = f32[64,32,256]{2,1,0:T(8,128)S(1)} fusion(f32[64,16,256]{2,1,0:T(8,128)S(1)} %bitcast.89, f32[64,16,256]{2,1,0:T(8,128)S(1)} %bitcast.87), kind=kOutput, calls=%fused_computation.16.clone.1 | convolution fusion | flops 201865216 | bytes 4194304 | tf_op jit(solution)/shard_map/while/body/eval_jaxpr/kn,snc->skc/dot_general | solution.py:55
  58.1 2.0 %fusion.284 = f32[64,32,256]{2,1,0:T(8,128)S(1)} fusion(f32[64,16,256]{2,1,0:T(8,128)S(1)} %bitcast.90, f32[64,16,256]{2,1,0:T(8,128)S(1)} %bitcast.88), kind=kOutput, calls=%fused_computation.17.clone.1 | convolution fusion | flops 201865216 | bytes 4194304 | tf_op jit(solution)/shard_map/while/body/eval_jaxpr/kn,snc->skc/dot_general | solution.py:56
  60.1 1.0 convolution_bitcast_fusion.9
  61.2 1.0 convolution_bitcast_fusion.8
  63.0 1.9 %fusion.286 = f32[64,32,256]{2,1,0:T(8,128)S(1)} fusion(f32[64,32,128]{2,1,0:T(8,128)S(1)} %get-tuple-element.512, f32[64,32,128]{2,1,0:T(8,128)S(1)} %get-tuple-element.513, f32[256,256]{1,0:T(8,128)S(1)} %get-tuple-element.544), kind=kOutput, calls=%fused_computation.10.clone.1 | convolution fusion | flops 1611137024 | bytes 4456448 | tf_op jit(solution)/shard_map/while/body/eval_jaxpr/skc,cd->skd/dot_general | solution.py:66
  64.9 1.9 %fusion.287 = f32[64,32,256]{2,1,0:T(8,128)S(1)} fusion(f32[64,32,128]{2,1,0:T(8,128)S(1)} %get-tuple-element.514, f32[64,32,128]{2,1,0:T(8,128)S(1)} %get-tuple-element.515, f32[256,256]{1,0:T(8,128)S(1)} %get-tuple-element.544), kind=kOutput, calls=%fused_computation.5.clone.1 | convolution fusion | flops 1611137024 | bytes 4456448 | tf_op jit(solution)/shard_map/while/body/eval_jaxpr/skc,cd->skd/dot_general | solution.py:66
  69.7 1.3 %copy.22 = f32[4,2,2048]{0,1,2:T(2,128)S(1)} copy(f32[4,2,2048]{2,0,1:T(4,128)S(1)} %pad_maximum_fusion.11) | data formatting | bytes 131072 | tf_op jit(solution)/shard_map/stack | solution.py:151
  71.0 3.8 %reshape.198 = f32[8,1,2048]{2,1,0:T(1,128)} reshape(f32[2048,2,4]{2,1,0:T(2,128)S(1)} %bitcast.93) | data formatting | bytes 131072
  74.8 7.3 %all-to-all-start = ((f32[8,1,2048]{2,1,0:T(1,128)}), f32[8,1,2048]{2,1,0:T(1,128)S(1)}, u32[]{:S(2)}, u32[]{:S(2)}) async-start(f32[8,1,2048]{2,1,0:T(1,128)} %reshape.198), calls=%async_computation | async-start | bytes 131072 | tf_op jit(solution)/shard_map/all_to_all | solution.py:150
  83.7 11.9 %all-reduce.1 = s32[32]{0:T(128)S(1)} all-reduce(s32[32]{0:T(128)S(1)} %dynamic-update-slice), channel_id=1, replica_groups=mesh['tm'=8,'chan'=4] {'tm'}, use_global_device_ids=true, to_apply=%add.1 | all-reduce | flops 32 | bytes 256
  97.6 3.2 %reshape.199 = f32[2048,2,4]{2,1,0:T(2,128)S(1)} reshape(f32[8,2048]{1,0:T(8,128)S(1)} %reduce.1) | data formatting | bytes 131072
  100.8 0.8 copy.26
  101.8 1.0 fusion.157
  110.6 3.4 %collective-permute-start = (f32[24,512]{1,0:T(8,128)S(1)}, f32[24,512]{1,0:T(8,128)S(1)}, u32[]{:S(2)}, u32[]{:S(2)}) collective-permute-start(f32[24,512]{1,0:T(8,128)S(1)} %get-tuple-element.415), channel_id=1, source_target_pairs={{0,4},{4,8},{8,12},{12,16},{16,20},{20,24},{24,28},{1,5},{5,9},{9,... | collective-permute-start | bytes 147464 | tf_op jit(solution)/shard_map/ppermute | solution.py:22
  114.0 1.5 %collective-permute-start.1 = (f32[24,512]{1,0:T(8,128)S(1)}, f32[24,512]{1,0:T(8,128)S(1)}, u32[]{:S(2)}, u32[]{:S(2)}) collective-permute-start(f32[24,512]{1,0:T(8,128)S(1)} %get-tuple-element.416), channel_id=1, source_target_pairs={{4,0},{8,4},{12,8},{16,12},{20,16},{24,20},{28,24},{5,1},{9,5},{13... | collective-permute-start | bytes 147464 | tf_op jit(solution)/shard_map/ppermute | solution.py:23
  115.7 4.3 %collective-permute-done.1 = f32[24,512]{1,0:T(8,128)S(1)} collective-permute-done((f32[24,512]{1,0:T(8,128)S(1)}, f32[24,512]{1,0:T(8,128)S(1)}, u32[]{:S(2)}, u32[]{:S(2)}) %collective-permute-start.1) | collective-permute-done | bytes 49184 | tf_op jit(solution)/shard_map/ppermute | solution.py:23
  120.0 6.7 %fusion.100 = f32[256,512]{1,0:T(8,128)} fusion(f32[24,512]{1,0:T(8,128)S(1)} %collective-permute-done.1, f32[256,512]{1,0:T(8,128)S(1)} %fusion.106, f32[24,512]{1,0:T(8,128)S(1)} %collective-permute-done, f32[256,1]{1,0:T(8,128)S(1)} %get-tuple-element.412, f32[256,511]{1,0:T(8,128)S(1)} %get-tuple-element.414, f32[256,511]{1,0:T(8,128)S(1)} %get-tuple-element.413, ...), kind=kOutput, calls=%fused_computation.128 | convolution fusion | flops 495104000 | bytes 26342592 | tf_op jit(solution)/shard_map/dot_general | solution.py:172
  (140 shorter events, 26.3 us)
Async XLA Ops:
  69.6 12.4 %copy-start.3 = (u32[32]{0:T(128)S(1)}, u32[32]{0:T(128)}, u32[]{:S(2)}) copy-start(u32[32]{0:T(128)} %constant.235) | copy-start | bytes 388
  69.7 13.8 %copy-start.2 = (s32[4]{0:T(128)S(1)}, s32[4]{0:T(128)}, u32[]{:S(2)}) copy-start(s32[4]{0:T(128)} %param.10) | copy-start | bytes 52
  69.7 25.9 %copy-start = (s32[256]{0:T(256)S(1)}, s32[256]{0:T(256)}, u32[]{:S(2)}) copy-start(s32[256]{0:T(256)} %param.12) | copy-start | bytes 3076
  69.7 25.9 %copy-start.1 = (s32[256]{0:T(256)S(1)}, s32[256]{0:T(256)}, u32[]{:S(2)}) copy-start(s32[256]{0:T(256)} %param.13) | copy-start | bytes 3076
  74.8 21.5 %all-to-all-start = ((f32[8,1,2048]{2,1,0:T(1,128)}), f32[8,1,2048]{2,1,0:T(1,128)S(1)}, u32[]{:S(2)}, u32[]{:S(2)}) async-start(f32[8,1,2048]{2,1,0:T(1,128)} %reshape.198), calls=%async_computation | async-start | bytes 131072 | tf_op jit(solution)/shard_map/all_to_all | solution.py:150
  110.6 5.1 %collective-permute-start = (f32[24,512]{1,0:T(8,128)S(1)}, f32[24,512]{1,0:T(8,128)S(1)}, u32[]{:S(2)}, u32[]{:S(2)}) collective-permute-start(f32[24,512]{1,0:T(8,128)S(1)} %get-tuple-element.415), channel_id=1, source_target_pairs={{0,4},{4,8},{8,12},{12,16},{16,20},{20,24},{24,28},{1,5},{5,9},{9,... | collective-permute-start | bytes 147464 | tf_op jit(solution)/shard_map/ppermute | solution.py:22
  114.0 6.0 %collective-permute-start.1 = (f32[24,512]{1,0:T(8,128)S(1)}, f32[24,512]{1,0:T(8,128)S(1)}, u32[]{:S(2)}, u32[]{:S(2)}) collective-permute-start(f32[24,512]{1,0:T(8,128)S(1)} %get-tuple-element.416), channel_id=1, source_target_pairs={{4,0},{8,4},{12,8},{16,12},{20,16},{24,20},{28,24},{5,1},{9,5},{13... | collective-permute-start | bytes 147464 | tf_op jit(solution)/shard_map/ppermute | solution.py:23
where the time goes:
time: 127 us
  matrix products  50.9 us (40%)
  local copies, waits for them, and re-layouts  28.4 us (22%)
  other arithmetic  17.3 us (14%)
  starting transfers between devices  12.2 us (10%)
  blocking collectives  11.9 us (9%)
  waiting for transfers between devices  4.46 us (4%)
    dot_general x8, matrix products, forward(): return jnp.einsum('skc,cd->skd', turned, mixer, precision=HIGH)  15.2 us
    dot_general x8, matrix products, forward(): second = jnp.einsum('kn,snc->skc', small_sin, signal, precision=HIGH)  12.2 us
    dot_general x8, matrix products, forward(): first = jnp.einsum('kn,snc->skc', small_cos, signal, precision=HIGH)  12.2 us
    unnamed x1, blocking collectives  11.9 us
    dynamic_slice x8, local copies, waits for them, and re-layouts, body(): lax.map(lambda item: correlate(item[0], item[1], item[2], tables), (surve...  9.53 us
    unnamed x15, local copies, waits for them, and re-layouts  7.96 us
    slice x48, local copies, waits for them, and re-layouts, body(): jnp.roll(power, step, axis=1)  7.45 us
    all_to_all x1, starting transfers between devices, body(): lax.all_to_all(jnp.stack([real_c, imag_c], axis=1), 'tm', split_axis=2, c...  7.27 us
  transfers between devices with their start and end apart: 3, of which 2 were waited for; matrix products, arithmetic and copies ran while one was open for 1% of the time, Pallas kernels for 0%

commit v1 on v0

--- a/solution.py
+++ b/solution.py
@@ -147,8 +147,14 @@
     real_c = corr[:, :, :128].reshape(blocks, D)
     imag_c = corr[:, :, 128:].reshape(blocks, D)
     norm = 1.0 / math.sqrt(total_blocks * SEGS * D)
-    moved = lax.all_to_all(
-        jnp.stack([real_c, imag_c], axis=1), "tm", split_axis=2, concat_axis=0, tiled=True
+    moved = jnp.concatenate(
+        lax.all_to_all(
+            jnp.stack(jnp.split(jnp.stack([real_c, imag_c], axis=1), lax.axis_size("tm"), axis=2)),
+            "tm",
+            0,
+            0,
+        ),
+        axis=0,
     )
     ids = lax.all_gather(block_ids, "tm", axis=0, tiled=True)
     stacked = jnp.concatenate([moved[:, 0], moved[:, 1]], 0)

time: 127 us -> 122 us (0.961)
  local copies, waits for them, and re-layouts: 28.4 us -> 18.7 us
  other arithmetic: 17.3 us -> 21.4 us
    unnamed x15 -> x13, local copies, waits for them, and re-layouts: 7.96 us -> 0.93 us
    unnamed x0 -> x7, other arithmetic: none -> 4.26 us
    all_to_all x3 -> x0, local copies, waits for them, and re-layouts: 1.39 us -> none  [body(): lax.all_to_all(jnp.stack([real_c, imag_c], axis=1), 'tm', split_axis=2, c...]
    another operation x3 -> x0, local copies, waits for them, and re-layouts: 1.32 us -> none  [body(): jnp.stack([real_c, imag_c], axis=1)]
where the time goes in v1:
time: 122 us; the launch traced here: 121 us
  matrix products  50.9 us (42%)
  other arithmetic  21.4 us (18%)
  local copies, waits for them, and re-layouts  18.7 us (15%)
  starting transfers between devices  12.2 us (10%)
  blocking collectives  11.9 us (10%)
  waiting for transfers between devices  4.4 us (4%)
    dot_general x8, matrix products, forward(): return jnp.einsum('skc,cd->skd', turned, mixer, precision=HIGH)  15.2 us
    dot_general x8, matrix products, forward(): second = jnp.einsum('kn,snc->skc', small_sin, signal, precision=HIGH)  12.2 us
    dot_general x8, matrix products, forward(): first = jnp.einsum('kn,snc->skc', small_cos, signal, precision=HIGH)  12.2 us
    unnamed x1, blocking collectives  11.9 us
    dynamic_slice x8, local copies, waits for them, and re-layouts, body(): lax.map(lambda item: correlate(item[0], item[1], item[2], tables), (surve...  9.54 us
    slice x48, local copies, waits for them, and re-layouts, body(): jnp.roll(power, step, axis=1)  7.45 us
    all_to_all x1, starting transfers between devices, body(): lax.all_to_all(jnp.stack(jnp.split(jnp.stack([real_c, imag_c], axis=1), l...  7.29 us
    dot_general x1, matrix products, body(): delay_sum = jnp.dot(band, padded, precision=HIGH)  6.73 us
  transfers between devices with their start and end apart: 3, of which 2 were waited for; matrix products, arithmetic and copies ran while one was open for 1% of the time, Pallas kernels for 0%

profile of v1, /device:TPU:0, one launch (start us, length us, event | category | flops | bytes accessed | tf_op | source)
XLA Modules:
  0.0 121.0 jit_solution(17058484985489234353)
XLA Ops:
  0.6 69.0 %while.15 = (s32[]{:T(128)}, f32[4,16,256]{2,1,0:T(8,128)S(1)}, s32[4]{0:T(128)}, bf16[4,1024,256]{2,1,0:T(8,128)(2,1)}, f32[256,256]{1,0:T(8,128)S(1)}, /*index...) while((s32[]{:T(128)}, f32[4,16,256]{2,1,0:T(8,128)S(1)}, s32[4]{0:T(128)}, ...), condition=%wide.region_3.4_spmd.clone.clone, body=%wide.region_0.3_spmd.clone.clone.sunk | while | flops 4067001856 | bytes 47000764 | solution.py:144
  0.6 1.3 %dynamic_slice.37 = s32[1]{0:T(128)} dynamic-slice(s32[4]{0:T(128)} %get-tuple-element.542, s32[]{:T(128)S(6)} %copy.21), dynamic_slice_sizes={1} | dynamic-slice | bytes 12 | tf_op jit(solution)/shard_map/while/body/jit(dynamic_index_in_dim)/dynamic_slice | solution.py:144
  2.0 1.1 constant_dynamic-slice_fusion.2
  3.1 1.1 dynamic-slice_convert_fusion.2
  4.4 2.0 %fusion.293 = f32[64,32,256]{2,1,0:T(8,128)S(1)} fusion(f32[64,16,256]{2,1,0:T(8,128)S(1)} %bitcast.104, f32[64,16,256]{2,1,0:T(8,128)S(1)} %bitcast.102), kind=kOutput, calls=%fused_computation.16.clone.1 | convolution fusion | flops 201865216 | bytes 4194304 | tf_op jit(solution)/shard_map/while/body/eval_jaxpr/kn,snc->skc/dot_general | solution.py:55
  6.4 2.0 %fusion.292 = f32[64,32,256]{2,1,0:T(8,128)S(1)} fusion(f32[64,16,256]{2,1,0:T(8,128)S(1)} %bitcast.105, f32[64,16,256]{2,1,0:T(8,128)S(1)} %bitcast.103), kind=kOutput, calls=%fused_computation.17.clone.1 | convolution fusion | flops 201865216 | bytes 4194304 | tf_op jit(solution)/shard_map/while/body/eval_jaxpr/kn,snc->skc/dot_general | solution.py:56
  8.5 1.0 convolution_bitcast_fusion.9
  9.5 1.0 convolution_bitcast_fusion.8
  10.6 0.8 multiply_add_fusion.7
  11.3 1.9 %fusion.294 = f32[64,32,256]{2,1,0:T(8,128)S(1)} fusion(f32[64,32,128]{2,1,0:T(8,128)S(1)} %get-tuple-element.512, f32[64,32,128]{2,1,0:T(8,128)S(1)} %get-tuple-element.513, f32[256,256]{1,0:T(8,128)S(1)} %get-tuple-element.544), kind=kOutput, calls=%fused_computation.10.clone.1 | convolution fusion | flops 1611137024 | bytes 4456448 | tf_op jit(solution)/shard_map/while/body/eval_jaxpr/skc,cd->skd/dot_general | solution.py:66
  13.2 1.9 %fusion.295 = f32[64,32,256]{2,1,0:T(8,128)S(1)} fusion(f32[64,32,128]{2,1,0:T(8,128)S(1)} %get-tuple-element.514, f32[64,32,128]{2,1,0:T(8,128)S(1)} %get-tuple-element.515, f32[256,256]{1,0:T(8,128)S(1)} %get-tuple-element.544), kind=kOutput, calls=%fused_computation.5.clone.1 | convolution fusion | flops 1611137024 | bytes 4456448 | tf_op jit(solution)/shard_map/while/body/eval_jaxpr/skc,cd->skd/dot_general | solution.py:66
  17.9 1.3 %dynamic_slice.37 = s32[1]{0:T(128)} dynamic-slice(s32[4]{0:T(128)} %get-tuple-element.542, s32[]{:T(128)S(6)} %copy.21), dynamic_slice_sizes={1} | dynamic-slice | bytes 12 | tf_op jit(solution)/shard_map/while/body/jit(dynamic_index_in_dim)/dynamic_slice | solution.py:144
  19.3 1.1 constant_dynamic-slice_fusion.2
  20.4 1.1 dynamic-slice_convert_fusion.2
  21.7 2.0 %fusion.293 = f32[64,32,256]{2,1,0:T(8,128)S(1)} fusion(f32[64,16,256]{2,1,0:T(8,128)S(1)} %bitcast.104, f32[64,16,256]{2,1,0:T(8,128)S(1)} %bitcast.102), kind=kOutput, calls=%fused_computation.16.clone.1 | convolution fusion | flops 201865216 | bytes 4194304 | tf_op jit(solution)/shard_map/while/body/eval_jaxpr/kn,snc->skc/dot_general | solution.py:55
  23.7 2.0 %fusion.292 = f32[64,32,256]{2,1,0:T(8,128)S(1)} fusion(f32[64,16,256]{2,1,0:T(8,128)S(1)} %bitcast.105, f32[64,16,256]{2,1,0:T(8,128)S(1)} %bitcast.103), kind=kOutput, calls=%fused_computation.17.clone.1 | convolution fusion | flops 201865216 | bytes 4194304 | tf_op jit(solution)/shard_map/while/body/eval_jaxpr/kn,snc->skc/dot_general | solution.py:56
  25.7 1.0 convolution_bitcast_fusion.9
  26.8 1.0 convolution_bitcast_fusion.8
  27.8 0.8 multiply_add_fusion.7
  28.6 1.9 %fusion.294 = f32[64,32,256]{2,1,0:T(8,128)S(1)} fusion(f32[64,32,128]{2,1,0:T(8,128)S(1)} %get-tuple-element.512, f32[64,32,128]{2,1,0:T(8,128)S(1)} %get-tuple-element.513, f32[256,256]{1,0:T(8,128)S(1)} %get-tuple-element.544), kind=kOutput, calls=%fused_computation.10.clone.1 | convolution fusion | flops 1611137024 | bytes 4456448 | tf_op jit(solution)/shard_map/while/body/eval_jaxpr/skc,cd->skd/dot_general | solution.py:66
  30.5 1.9 %fusion.295 = f32[64,32,256]{2,1,0:T(8,128)S(1)} fusion(f32[64,32,128]{2,1,0:T(8,128)S(1)} %get-tuple-element.514, f32[64,32,128]{2,1,0:T(8,128)S(1)} %get-tuple-element.515, f32[256,256]{1,0:T(8,128)S(1)} %get-tuple-element.544), kind=kOutput, calls=%fused_computation.5.clone.1 | convolution fusion | flops 1611137024 | bytes 4456448 | tf_op jit(solution)/shard_map/while/body/eval_jaxpr/skc,cd->skd/dot_general | solution.py:66
  35.1 1.3 %dynamic_slice.37 = s32[1]{0:T(128)} dynamic-slice(s32[4]{0:T(128)} %get-tuple-element.542, s32[]{:T(128)S(6)} %copy.21), dynamic_slice_sizes={1} | dynamic-slice | bytes 12 | tf_op jit(solution)/shard_map/while/body/jit(dynamic_index_in_dim)/dynamic_slice | solution.py:144
  36.5 1.1 constant_dynamic-slice_fusion.2
  37.6 1.1 dynamic-slice_convert_fusion.2
  38.9 2.0 %fusion.293 = f32[64,32,256]{2,1,0:T(8,128)S(1)} fusion(f32[64,16,256]{2,1,0:T(8,128)S(1)} %bitcast.104, f32[64,16,256]{2,1,0:T(8,128)S(1)} %bitcast.102), kind=kOutput, calls=%fused_computation.16.clone.1 | convolution fusion | flops 201865216 | bytes 4194304 | tf_op jit(solution)/shard_map/while/body/eval_jaxpr/kn,snc->skc/dot_general | solution.py:55
  40.9 2.0 %fusion.292 = f32[64,32,256]{2,1,0:T(8,128)S(1)} fusion(f32[64,16,256]{2,1,0:T(8,128)S(1)} %bitcast.105, f32[64,16,256]{2,1,0:T(8,128)S(1)} %bitcast.103), kind=kOutput, calls=%fused_computation.17.clone.1 | convolution fusion | flops 201865216 | bytes 4194304 | tf_op jit(solution)/shard_map/while/body/eval_jaxpr/kn,snc->skc/dot_general | solution.py:56
  42.9 1.0 convolution_bitcast_fusion.9
  44.0 1.1 convolution_bitcast_fusion.8
  45.1 0.8 multiply_add_fusion.7
  45.8 1.9 %fusion.294 = f32[64,32,256]{2,1,0:T(8,128)S(1)} fusion(f32[64,32,128]{2,1,0:T(8,128)S(1)} %get-tuple-element.512, f32[64,32,128]{2,1,0:T(8,128)S(1)} %get-tuple-element.513, f32[256,256]{1,0:T(8,128)S(1)} %get-tuple-element.544), kind=kOutput, calls=%fused_computation.10.clone.1 | convolution fusion | flops 1611137024 | bytes 4456448 | tf_op jit(solution)/shard_map/while/body/eval_jaxpr/skc,cd->skd/dot_general | solution.py:66
  47.7 1.9 %fusion.295 = f32[64,32,256]{2,1,0:T(8,128)S(1)} fusion(f32[64,32,128]{2,1,0:T(8,128)S(1)} %get-tuple-element.514, f32[64,32,128]{2,1,0:T(8,128)S(1)} %get-tuple-element.515, f32[256,256]{1,0:T(8,128)S(1)} %get-tuple-element.544), kind=kOutput, calls=%fused_computation.5.clone.1 | convolution fusion | flops 1611137024 | bytes 4456448 | tf_op jit(solution)/shard_map/while/body/eval_jaxpr/skc,cd->skd/dot_general | solution.py:66
  52.4 1.3 %dynamic_slice.37 = s32[1]{0:T(128)} dynamic-slice(s32[4]{0:T(128)} %get-tuple-element.542, s32[]{:T(128)S(6)} %copy.21), dynamic_slice_sizes={1} | dynamic-slice | bytes 12 | tf_op jit(solution)/shard_map/while/body/jit(dynamic_index_in_dim)/dynamic_slice | solution.py:144
  53.8 1.1 constant_dynamic-slice_fusion.2
  54.9 1.1 dynamic-slice_convert_fusion.2
  56.2 2.0 %fusion.293 = f32[64,32,256]{2,1,0:T(8,128)S(1)} fusion(f32[64,16,256]{2,1,0:T(8,128)S(1)} %bitcast.104, f32[64,16,256]{2,1,0:T(8,128)S(1)} %bitcast.102), kind=kOutput, calls=%fused_computation.16.clone.1 | convolution fusion | flops 201865216 | bytes 4194304 | tf_op jit(solution)/shard_map/while/body/eval_jaxpr/kn,snc->skc/dot_general | solution.py:55
  58.2 2.0 %fusion.292 = f32[64,32,256]{2,1,0:T(8,128)S(1)} fusion(f32[64,16,256]{2,1,0:T(8,128)S(1)} %bitcast.105, f32[64,16,256]{2,1,0:T(8,128)S(1)} %bitcast.103), kind=kOutput, calls=%fused_computation.17.clone.1 | convolution fusion | flops 201865216 | bytes 4194304 | tf_op jit(solution)/shard_map/while/body/eval_jaxpr/kn,snc->skc/dot_general | solution.py:56
  60.2 1.0 convolution_bitcast_fusion.9
  61.2 1.0 convolution_bitcast_fusion.8
  62.3 0.8 multiply_add_fusion.7
  63.1 1.9 %fusion.294 = f32[64,32,256]{2,1,0:T(8,128)S(1)} fusion(f32[64,32,128]{2,1,0:T(8,128)S(1)} %get-tuple-element.512, f32[64,32,128]{2,1,0:T(8,128)S(1)} %get-tuple-element.513, f32[256,256]{1,0:T(8,128)S(1)} %get-tuple-element.544), kind=kOutput, calls=%fused_computation.10.clone.1 | convolution fusion | flops 1611137024 | bytes 4456448 | tf_op jit(solution)/shard_map/while/body/eval_jaxpr/skc,cd->skd/dot_general | solution.py:66
  65.0 1.9 %fusion.295 = f32[64,32,256]{2,1,0:T(8,128)S(1)} fusion(f32[64,32,128]{2,1,0:T(8,128)S(1)} %get-tuple-element.514, f32[64,32,128]{2,1,0:T(8,128)S(1)} %get-tuple-element.515, f32[256,256]{1,0:T(8,128)S(1)} %get-tuple-element.544), kind=kOutput, calls=%fused_computation.5.clone.1 | convolution fusion | flops 1611137024 | bytes 4456448 | tf_op jit(solution)/shard_map/while/body/eval_jaxpr/skc,cd->skd/dot_general | solution.py:66
  74.5 7.3 %all-to-all-start = ((f32[8,4,2,256]{3,2,1,0:T(2,128)}), f32[8,4,2,256]{3,2,1,0:T(2,128)S(1)}, u32[]{:S(2)}, u32[]{:S(2)}) async-start(f32[8,4,2,256]{3,2,1,0:T(2,128)} %constant_dynamic-update-slice_fusion), calls=%async_computation | async-start | bytes 131072 | tf_op jit(solution)/shard_map/all_to_all | solution.py:151
  83.4 11.9 %all-reduce.1 = s32[32]{0:T(128)S(1)} all-reduce(s32[32]{0:T(128)S(1)} %dynamic-update-slice), channel_id=1, replica_groups=mesh['tm'=8,'chan'=4] {'tm'}, use_global_device_ids=true, to_apply=%add.1 | all-reduce | flops 32 | bytes 256
  96.1 1.0 fusion.157
  104.9 3.4 %collective-permute-start = (f32[24,512]{1,0:T(8,128)S(1)}, f32[24,512]{1,0:T(8,128)S(1)}, u32[]{:S(2)}, u32[]{:S(2)}) collective-permute-start(f32[24,512]{1,0:T(8,128)S(1)} %get-tuple-element.415), channel_id=1, source_target_pairs={{0,4},{4,8},{8,12},{12,16},{16,20},{20,24},{24,28},{1,5},{5,9},{9,... | collective-permute-start | bytes 147464 | tf_op jit(solution)/shard_map/ppermute | solution.py:22
  108.3 1.5 %collective-permute-start.1 = (f32[24,512]{1,0:T(8,128)S(1)}, f32[24,512]{1,0:T(8,128)S(1)}, u32[]{:S(2)}, u32[]{:S(2)}) collective-permute-start(f32[24,512]{1,0:T(8,128)S(1)} %get-tuple-element.416), channel_id=1, source_target_pairs={{4,0},{8,4},{12,8},{16,12},{20,16},{24,20},{28,24},{5,1},{9,5},{13... | collective-permute-start | bytes 147464 | tf_op jit(solution)/shard_map/ppermute | solution.py:23
  110.0 4.3 %collective-permute-done.1 = f32[24,512]{1,0:T(8,128)S(1)} collective-permute-done((f32[24,512]{1,0:T(8,128)S(1)}, f32[24,512]{1,0:T(8,128)S(1)}, u32[]{:S(2)}, u32[]{:S(2)}) %collective-permute-start.1) | collective-permute-done | bytes 49184 | tf_op jit(solution)/shard_map/ppermute | solution.py:23
  114.2 6.7 %fusion.100 = f32[256,512]{1,0:T(8,128)} fusion(f32[24,512]{1,0:T(8,128)S(1)} %collective-permute-done.1, f32[256,512]{1,0:T(8,128)S(1)} %fusion.106, f32[24,512]{1,0:T(8,128)S(1)} %collective-permute-done, f32[256,1]{1,0:T(8,128)S(1)} %get-tuple-element.412, f32[256,511]{1,0:T(8,128)S(1)} %get-tuple-element.414, f32[256,511]{1,0:T(8,128)S(1)} %get-tuple-element.413, ...), kind=kOutput, calls=%fused_computation.128 | convolution fusion | flops 495104000 | bytes 26342592 | tf_op jit(solution)/shard_map/dot_general | solution.py:178
  (138 shorter events, 26.7 us)
Async XLA Ops:
  0.6 81.2 %copy-start.3 = (u32[32]{0:T(128)S(1)}, u32[32]{0:T(128)}, u32[]{:S(2)}) copy-start(u32[32]{0:T(128)} %constant.235) | copy-start | bytes 388
  0.6 82.6 %copy-start.2 = (s32[4]{0:T(128)S(1)}, s32[4]{0:T(128)}, u32[]{:S(2)}) copy-start(s32[4]{0:T(128)} %param.10) | copy-start | bytes 52
  0.6 94.7 %copy-start = (s32[256]{0:T(256)S(1)}, s32[256]{0:T(256)}, u32[]{:S(2)}) copy-start(s32[256]{0:T(256)} %param.12) | copy-start | bytes 3076
  0.6 94.7 %copy-start.1 = (s32[256]{0:T(256)S(1)}, s32[256]{0:T(256)}, u32[]{:S(2)}) copy-start(s32[256]{0:T(256)} %param.13) | copy-start | bytes 3076
  74.5 21.5 %all-to-all-start = ((f32[8,4,2,256]{3,2,1,0:T(2,128)}), f32[8,4,2,256]{3,2,1,0:T(2,128)S(1)}, u32[]{:S(2)}, u32[]{:S(2)}) async-start(f32[8,4,2,256]{3,2,1,0:T(2,128)} %constant_dynamic-update-slice_fusion), calls=%async_computation | async-start | bytes 131072 | tf_op jit(solution)/shard_map/all_to_all | solution.py:151
  104.9 5.1 %collective-permute-start = (f32[24,512]{1,0:T(8,128)S(1)}, f32[24,512]{1,0:T(8,128)S(1)}, u32[]{:S(2)}, u32[]{:S(2)}) collective-permute-start(f32[24,512]{1,0:T(8,128)S(1)} %get-tuple-element.415), channel_id=1, source_target_pairs={{0,4},{4,8},{8,12},{12,16},{16,20},{20,24},{24,28},{1,5},{5,9},{9,... | collective-permute-start | bytes 147464 | tf_op jit(solution)/shard_map/ppermute | solution.py:22
  108.3 6.0 %collective-permute-start.1 = (f32[24,512]{1,0:T(8,128)S(1)}, f32[24,512]{1,0:T(8,128)S(1)}, u32[]{:S(2)}, u32[]{:S(2)}) collective-permute-start(f32[24,512]{1,0:T(8,128)S(1)} %get-tuple-element.416), channel_id=1, source_target_pairs={{4,0},{8,4},{12,8},{16,12},{20,16},{24,20},{28,24},{5,1},{9,5},{13... | collective-permute-start | bytes 147464 | tf_op jit(solution)/shard_map/ppermute | solution.py:23
